TPU v7x, 32 devices: a whole 2x2x4 slice. The times are simulated.
32 devices in a mesh: seq: 8 (over z, x), chan: 4 (over y, core).
Axes of the slice: x: 2, y: 2, z: 4, core: 2. Of those that a mesh axis runs over, the one named last changes fastest.
Arguments:
- hidden: bfloat16 [8, 8192], replicated, may hold values from -6 to 6
- norm_gain: float32 [3, 8192], replicated, may hold values from 0.25 to 1.75
- in_weight: bfloat16 [2, 8192, 2, 16384], P(None, None, None, ('seq', 'chan')), may hold values from -0.125 to 0.125
- conv_weight: float32 [2, 4, 16384], P(None, None, ('seq', 'chan')), may hold values from -3 to 3
- conv_bias: float32 [2, 16384], P(None, ('seq', 'chan')), may hold values from -3 to 3
- conv_state: bfloat16 [2, 8, 3, 16384], P(None, None, None, ('seq', 'chan')), may hold values from -6 to 6
- xproj_weight: bfloat16 [2, 16384, 544], P(None, ('seq', 'chan')), may hold values from -0.09375 to 0.09375
- dt_weight: bfloat16 [2, 512, 16384], P(None, None, ('seq', 'chan')), may hold values from -0.25 to 0.25
- dt_bias: float32 [2, 16384], P(None, ('seq', 'chan')), may hold values from -4.6 to -2.3
- a_log: float32 [2, 16, 16384], P(None, None, ('seq', 'chan')), may hold values from 0 to 2.77
- skip_gain: float32 [2, 16384], P(None, ('seq', 'chan')), may hold values from 0.5 to 1.5
- ssm_state: float32 [2, 8, 16, 16384], P(None, None, None, ('seq', 'chan')), may hold values from -6 to 6
- out_weight: bfloat16 [2, 16384, 8192], P(None, ('seq', 'chan')), may hold values from -0.09375 to 0.09375
- asker_lookup_matrix: bfloat16 [8192, 8, 1280], P('seq', 'chan'), may hold values from -0.0625 to 0.0625
- o_weight: bfloat16 [8, 1024, 8192], P('chan', None, 'seq'), may hold values from -0.09375 to 0.09375
- kv_cache: bfloat16 [64, 256, 2, 8, 128], P('seq', None, None, 'chan'), may hold values from -64 to 64
- lengths: int32 [8], replicated, may hold values from 1 to 2048, as said below
- page_table: int32 [8, 8], replicated, may hold values from -1 to 63, as said below
Outputs:
- hidden_out: bfloat16 [8, 8192], P(None, ('seq', 'chan'))
- new_ssm: float32 [2, 8, 16, 16384], P(None, None, None, ('seq', 'chan'))
- new_conv: bfloat16 [2, 8, 3, 16384], P(None, None, None, ('seq', 'chan'))
- newest_pair: bfloat16 [8, 8, 2, 128], P(None, 'chan')
Inputs may be any that keep to these rules, and one draw needn't show every extreme that they name: `lengths`: each request's context holds 1 to 2048 tokens; one request holds exactly 2048. page_table[b, j] for j < ceil(lengths[b] / 256) is the cache slot (index along seq times 8 plus the local slot) holding block j of request b; these slots are all different; every other entry is -1. Used slots are spread very unevenly: some devices along seq have all 8 of theirs used, others few or none.
All inputs are finite; a program needn't handle non-finite values.
Results may differ from a plain program's by a relative error of at most 0.018.
Values may be sent and summed in bfloat16 or wider, within the bound.
A program may use at most 192 MiB of HBM per device.

v0:
```python
import jax
import jax.numpy as jnp
from jax import lax
from jax.sharding import PartitionSpec as P

norm_eps = 1e-06
lowest_score = -1e30


def normalize(stream, gain_row):
    widened = stream.astype(jnp.float32)
    inv_rms = lax.rsqrt(jnp.mean(widened * widened, axis=1) + norm_eps)
    return (widened * inv_rms[:, None] * gain_row[None, :]).astype(jnp.bfloat16)


def mamba_mix(normed, layer, params):
    (
        in_weight,
        conv_weight,
        conv_bias,
        conv_state,
        xproj_weight,
        dt_weight,
        dt_bias,
        a_log,
        skip_gain,
        ssm_state,
    ) = params
    channels = in_weight.shape[3]
    both_proj = jnp.dot(
        normed,
        in_weight[layer].reshape(in_weight.shape[1], 2 * channels),
        preferred_element_type=jnp.float32,
    ).astype(jnp.bfloat16)
    inputs = both_proj[:, :channels]
    gate_half = both_proj[:, channels:]
    window = jnp.concatenate([conv_state[layer], inputs[:, None, :]], axis=1)
    conv_sum = (
        jnp.sum(window.astype(jnp.float32) * conv_weight[layer][None], axis=1)
        + conv_bias[layer][None, :]
    )
    signal = lax.optimization_barrier(jax.nn.silu(conv_sum).astype(jnp.bfloat16))
    x_terms = jnp.dot(signal, xproj_weight[layer], preferred_element_type=jnp.float32)
    mapped_vectors = lax.psum(x_terms, ("seq", "chan"))
    low_rank = dt_weight.shape[1]
    state_size = a_log.shape[1]
    dt_low = mapped_vectors[:, :low_rank].astype(jnp.bfloat16)
    b_in = mapped_vectors[:, low_rank : low_rank + state_size]
    c_out = mapped_vectors[:, low_rank + state_size :]
    dt_step = jax.nn.softplus(
        jnp.dot(dt_low, dt_weight[layer], preferred_element_type=jnp.float32)
        + dt_bias[layer][None, :]
    )
    widened = signal.astype(jnp.float32)
    decay_rate = jnp.exp(-dt_step[:, None, :] * jnp.exp(a_log[layer])[None])
    fresh_state = decay_rate * ssm_state[layer] + (dt_step * widened)[:, None, :] * b_in[:, :, None]
    readout = jnp.sum(fresh_state * c_out[:, :, None], axis=1) + skip_gain[layer][None, :] * widened
    gated_out = (readout * jax.nn.silu(gate_half.astype(jnp.float32))).astype(jnp.bfloat16)
    return (gated_out, fresh_state, window[:, 1:, :])


def mix_out(gated_out, out_weight, layer):
    weights_now = out_weight[layer]
    summed = lax.psum(
        jnp.dot(gated_out, weights_now, preferred_element_type=jnp.float32), ("seq", "chan")
    )
    return summed


def attend(normed, asker_lookup_matrix, kv_cache, lengths, page_table):
    requests = normed.shape[0]
    heads_kv = asker_lookup_matrix.shape[1]
    per_lens_width = kv_cache.shape[4]
    group_size = asker_lookup_matrix.shape[2] // per_lens_width - 2
    inv_sqrt = per_lens_width ** (-0.5)
    qkv_terms = jnp.einsum(
        "bd,dkc->bkc", normed, asker_lookup_matrix, preferred_element_type=jnp.float32
    )
    qkv_all = lax.optimization_barrier(lax.psum(qkv_terms, "seq").astype(jnp.bfloat16))
    every_question = qkv_all[:, :, : group_size * per_lens_width].reshape(
        requests, heads_kv, group_size, per_lens_width
    )
    newest_pair = qkv_all[:, :, group_size * per_lens_width :].reshape(
        requests, heads_kv, 2, per_lens_width
    )
    pages_dev = kv_cache.shape[0]
    block_len = kv_cache.shape[1]
    slot_ids = lax.axis_index("seq") * pages_dev + jnp.arange(pages_dev, dtype=jnp.int32)
    matches = page_table[:, :, None] == slot_ids[None, None, :]
    belongs = jnp.any(matches, axis=1)
    in_use = jnp.any(belongs, axis=0)
    owner_req = jnp.sum(
        jnp.where(belongs, jnp.arange(requests, dtype=jnp.int32)[:, None], 0), axis=0
    )
    page_index = jnp.sum(
        jnp.where(matches, jnp.arange(page_table.shape[1], dtype=jnp.int32)[None, :, None], 0),
        axis=(0, 1),
    )
    filled = jnp.where(
        in_use, jnp.clip(lengths[owner_req] - page_index * block_len, 0, block_len), 0
    )
    live_count = jnp.sum(in_use.astype(jnp.int32))
    per_step = max(1, 512 // block_len)
    padded = -(-pages_dev // per_step) * per_step
    slot_order = jnp.argsort(
        jnp.where(in_use, 0, pages_dev) + jnp.arange(pages_dev, dtype=jnp.int32)
    )
    slot_order = jnp.concatenate([slot_order, jnp.zeros((padded - pages_dev,), jnp.int32)])
    live_lane = jnp.arange(padded, dtype=jnp.int32) < live_count
    lane_fill = jnp.where(live_lane, filled[slot_order], 0)
    lane_owner = owner_req[slot_order]

    def visit(index_step, carried):
        page_tops, page_sums, page_accs = carried
        first_lane = index_step * per_step
        slots_now = lax.dynamic_slice_in_dim(slot_order, first_lane, per_step)
        fills_now = lax.dynamic_slice_in_dim(lane_fill, first_lane, per_step)
        owners_now = lax.dynamic_slice_in_dim(lane_owner, first_lane, per_step)
        page_rows = kv_cache[slots_now]
        queries = every_question[owners_now]
        scores = (
            jnp.einsum(
                "pkgd,ptkd->pkgt", queries, page_rows[:, :, 0], preferred_element_type=jnp.float32
            )
            * inv_sqrt
        )
        visible = (
            jnp.arange(block_len, dtype=jnp.int32)[None, None, None, :]
            < fills_now[:, None, None, None]
        )
        scores = jnp.where(visible, scores, lowest_score)
        block_top = jnp.max(scores, axis=3)
        weight = jnp.where(visible, jnp.exp(scores - block_top[..., None]), 0.0)
        block_sum = jnp.sum(weight, axis=3)
        values = jnp.einsum(
            "pkgt,ptkd->pkgd",
            weight.astype(jnp.bfloat16),
            page_rows[:, :, 1],
            preferred_element_type=jnp.float32,
        )
        return (
            lax.dynamic_update_slice_in_dim(page_tops, block_top, first_lane, 0),
            lax.dynamic_update_slice_in_dim(page_sums, block_sum, first_lane, 0),
            lax.dynamic_update_slice_in_dim(page_accs, values, first_lane, 0),
        )

    start_state = (
        jnp.full((padded, heads_kv, group_size), lowest_score, jnp.float32),
        jnp.zeros((padded, heads_kv, group_size), jnp.float32),
        jnp.zeros((padded, heads_kv, group_size, per_lens_width), jnp.float32),
    )
    step_count = (live_count + per_step - 1) // per_step
    page_tops, page_sums, page_accs = lax.fori_loop(0, step_count, visit, start_state)
    selects = (lane_owner[None, :] == jnp.arange(requests, dtype=jnp.int32)[:, None]) & live_lane[
        None, :
    ]
    chosen = selects[:, :, None, None]
    local_top = jnp.max(jnp.where(chosen, page_tops[None], lowest_score), axis=1)
    factor = jnp.where(chosen, jnp.exp(page_tops[None] - local_top[:, None]), 0.0)
    local_sum = jnp.sum(factor * page_sums[None], axis=1)
    local_acc = jnp.einsum("bpkg,pkgd->bkgd", factor, page_accs, precision=lax.Precision.HIGHEST)
    grand_top = lax.pmax(local_top, "seq")
    rescale = jnp.exp(local_top - grand_top)
    weight_total, value_total = (
        lax.psum((local_sum * rescale).astype(jnp.bfloat16), "seq").astype(jnp.float32),
        lax.psum((local_acc * rescale[..., None]).astype(jnp.bfloat16), "seq").astype(jnp.float32),
    )
    fresh_score = (
        jnp.einsum(
            "ujqf,ujf->ujq",
            every_question,
            newest_pair[:, :, 0],
            preferred_element_type=jnp.float32,
        )
        * inv_sqrt
    )
    final_top = jnp.maximum(grand_top, fresh_score)
    carry_old = jnp.exp(grand_top - final_top)
    fresh_weight = jnp.exp(fresh_score - final_top)
    denominator = weight_total * carry_old + fresh_weight
    numerator = value_total * carry_old[..., None] + fresh_weight[..., None] * newest_pair[:, :, 1][
        :, :, None, :
    ].astype(jnp.float32)
    attended = (numerator / denominator[..., None]).astype(jnp.bfloat16)
    return (attended.reshape(requests, heads_kv, group_size * per_lens_width), newest_pair)


def shards(
    hidden,
    norm_gain,
    in_weight,
    conv_weight,
    conv_bias,
    conv_state,
    xproj_weight,
    dt_weight,
    dt_bias,
    a_log,
    skip_gain,
    ssm_state,
    out_weight,
    asker_lookup_matrix,
    o_weight,
    kv_cache,
    lengths,
    page_table,
):
    layer_params = (
        in_weight,
        conv_weight,
        conv_bias,
        conv_state,
        xproj_weight,
        dt_weight,
        dt_bias,
        a_log,
        skip_gain,
        ssm_state,
    )
    model_dim = hidden.shape[1]
    share_cols = model_dim // lax.axis_size(("seq", "chan"))
    block_cols = model_dim // lax.axis_size("seq")
    seq_index = lax.axis_index("seq")
    share_index = seq_index * lax.axis_size("chan") + lax.axis_index("chan")
    normed = normalize(hidden, norm_gain[0])
    gated_first, state_first, conv_first = mamba_mix(normed, 0, layer_params)
    stream_full = (hidden.astype(jnp.float32) + mix_out(gated_first, out_weight, 0)).astype(
        jnp.bfloat16
    )
    stream_one = lax.dynamic_slice_in_dim(stream_full, share_index * share_cols, share_cols, 1)
    widened = stream_full.astype(jnp.float32)
    inv_rms = lax.rsqrt(jnp.mean(widened * widened, axis=1) + norm_eps)
    block_rows = lax.dynamic_slice_in_dim(widened, seq_index * block_cols, block_cols, 1)
    gain_block = lax.dynamic_slice_in_dim(norm_gain[1], seq_index * block_cols, block_cols, 0)
    attn_in = (block_rows * inv_rms[:, None] * gain_block[None, :]).astype(jnp.bfloat16)
    attended, newest_pair = attend(attn_in, asker_lookup_matrix, kv_cache, lengths, page_table)
    attn_share = lax.psum_scatter(
        jnp.einsum("khc,bkh->cb", o_weight, attended, preferred_element_type=jnp.float32),
        "chan",
        scatter_dimension=0,
        tiled=True,
    )
    stream_two = (stream_one.astype(jnp.float32) + attn_share.T).astype(jnp.bfloat16)
    normed_two = normalize(
        lax.all_gather(stream_two, ("seq", "chan"), axis=1, tiled=True), norm_gain[2]
    )
    gated_two, state_two, conv_two = mamba_mix(normed_two, 1, layer_params)
    added = lax.dynamic_slice_in_dim(
        mix_out(gated_two, out_weight, 1), share_index * share_cols, share_cols, 1
    )
    hidden_out = (stream_two.astype(jnp.float32) + added).astype(jnp.bfloat16)
    return (
        hidden_out,
        jnp.stack([state_first, state_two]),
        jnp.stack([conv_first, conv_two]),
        newest_pair,
    )


def solution(mesh):
    in_specs = (
        P(),
        P(),
        P(None, None, None, ("seq", "chan")),
        P(None, None, ("seq", "chan")),
        P(None, ("seq", "chan")),
        P(None, None, None, ("seq", "chan")),
        P(None, ("seq", "chan"), None),
        P(None, None, ("seq", "chan")),
        P(None, ("seq", "chan")),
        P(None, None, ("seq", "chan")),
        P(None, ("seq", "chan")),
        P(None, None, None, ("seq", "chan")),
        P(None, ("seq", "chan"), None),
        P("seq", "chan", None),
        P("chan", None, "seq"),
        P("seq", None, None, "chan", None),
        P(),
        P(),
    )
    out_specs = (
        P(None, ("seq", "chan")),
        P(None, None, None, ("seq", "chan")),
        P(None, None, None, ("seq", "chan")),
        P(None, "chan", None, None),
    )
    return jax.shard_map(shards, mesh=mesh, in_specs=in_specs, out_specs=out_specs, check_vma=False)
```

profile of v0, /device:TPU:0, one launch (start us, length us, event | category | flops | bytes accessed | tf_op | source)
XLA Modules:
  0.0 578.4 jit_solution(4350109685984095910)
XLA Ops:
  7.2 25.8 %fusion.107 = (bf16[1,8192,2,512]{3,2,1,0:T(2,128)(2,1)S(1)}, bf16[1,8192,2,512]{3,2,1,0:T(2,128)(2,1)}) fusion(bf16[2,8192,2,512]{3,2,1,0:T(2,128)(2,1)} %param.22), kind=kLoop, calls=%fused_computation.194 | loop fusion | bytes 67108864 | tf_op jit(solution)/shard_map/slice | solution.py:32
  33.1 3.0 copy.60
  36.1 0.7 fusion.108
  36.8 0.2 fusion.32
  37.1 2.3 convolution_convert_fusion.1
  39.5 0.6 slice_bitcast_fusion.10
  40.1 0.6 fusion.115
  40.7 0.2 fusion.21
  41.0 42.1 %psum.49 = f32[8,544]{1,0:T(8,128)S(1)} all-reduce(f32[8,544]{1,0:T(8,128)S(1)} %fusion.21), channel_id=1, replica_groups=mesh['seq'=8,'chan'=4] {'seq','chan'}, use_global_device_ids=true, to_apply=%region_2.3 | all-reduce | flops 4352 | bytes 34816 | tf_op jit(solution)/shard_map/psum | solution.py:44
  83.2 0.5 fusion.114
  83.7 0.5 fusion.113
  84.3 0.2 fusion.112
  84.7 5.3 fusion.11
  90.3 0.6 gather_fusion.2
  90.9 0.7 iota_add_fusion
  91.7 1.0 sort.17
  92.6 0.6 compare_select_fusion.5
  93.2 1.2 gather_fusion.4
  94.4 0.6 gather_fusion.3
  95.0 0.7 iota_compare_fusion.2
  95.7 1.2 fusion.97
  96.9 1.3 broadcast_select_fusion
  98.9 16.6 %copy.61 = bf16[1024,8,2,512]{3,1,2,0:T(8,128)(2,1)} copy(bf16[1024,8,2,512]{3,2,1,0:T(2,128)(2,1)} %bitcast.149) | data formatting | bytes 33554432
  115.5 2.1 copy.41
  117.7 0.7 constant_dynamic-slice_fusion
  118.4 98.2 %all-reduce.4.cloned.1.call-done = f32[8,8192]{1,0:T(8,128)} async-done(((f32[8,8192]{1,0:T(8,128)}), f32[8,8192]{1,0:T(8,128)}) %all-reduce.4.cloned.1.call-update) | async-done | bytes 262160 | tf_op jit(solution)/shard_map/psum | solution.py:64
  216.6 1.1 multiply_reduce_fusion
  217.8 3.3 fusion.15
  221.1 37.3 %psum.51 = bf16[8,2,1280]{2,0,1:T(8,128)(2,1)S(1)} all-reduce(f32[8,2,1280]{2,0,1:T(8,128)S(1)} %fusion.15), channel_id=1, replica_groups=mesh['seq'=8,'chan'=4] {'seq'}, use_global_device_ids=true, to_apply=%region_12.13 | all-reduce | flops 20480 | bytes 122880 | tf_op jit(solution)/shard_map/psum | solution.py:79
  258.5 0.6 broadcast_in_dim.149.clone
  259.1 8.1 %while.14 = (s32[]{:T(128)}, f32[8,2,8]{2,1,0:T(2,128)S(1)}, f32[8,2,8]{2,1,0:T(2,128)S(1)}, f32[8,2,8,128]{3,0,2,1:T(8,128)}, s32[]{:T(128)}, /*index=5*/s32[8]...) while((s32[]{:T(128)}, f32[8,2,8]{2,1,0:T(2,128)S(1)}, ...), condition=%wide.region_16.17_spmd, body=%wide.region_13.16_spmd.sunk | while | flops 4270546 | bytes 1767079 | solution.py:153
  259.1 0.7 compare_select_fusion.8
  259.8 0.6 gather_fusion
  260.4 0.6 gather_fusion.1
  261.1 0.7 dynamic_slice.37
  261.9 0.2 fusion.131
  262.3 0.2 fusion.133
  262.5 0.6 copy_dynamic-update-slice_fusion.2
  263.2 0.7 compare_select_fusion.8
  263.9 0.6 gather_fusion
  264.5 0.6 gather_fusion.1
  265.1 0.7 dynamic_slice.37
  265.9 0.2 fusion.131
  266.4 0.2 fusion.133
  266.6 0.6 copy_dynamic-update-slice_fusion.2
  267.4 0.7 select_reduce_fusion
  268.1 25.2 %pmax.7 = f32[8,2,8]{0,2,1:T(8,128)S(1)} all-reduce(f32[8,2,8]{0,2,1:T(8,128)S(1)} %select_reduce_fusion), channel_id=1, replica_groups=mesh['seq'=8,'chan'=4] {'seq'}, use_global_device_ids=true, to_apply=%region_18.19 | all-reduce | flops 128 | bytes 1024 | tf_op jit(solution)/shard_map/pmax | solution.py:162
  293.3 0.8 multiply_reduce_fusion.2
  294.4 1.2 fusion.18
  295.5 33.4 %all-reduce = (bf16[8,2,8,128]{3,0,2,1:T(8,128)(2,1)S(1)}, bf16[8,2,8]{0,2,1:T(8,128)(2,1)S(1)}) all-reduce(bf16[8,2,8,128]{3,0,2,1:T(8,128)(2,1)S(1)} %fusion.18, bf16[8,2,8]{0,2,1:T(8,128)(2,1)S(1)} %get-tuple-element.133), channel_id=1, replica_groups=mesh['seq'=8,'chan'=4] {'seq'}, use_global_device_ids=true, to_apply=%region_19.20 | all-reduce | flops 16512 | bytes 66048 | tf_op jit(solution)/shard_map/psum | solution.py:166
  328.9 3.5 convolution_bitcast_fusion.1
  332.5 1.3 copy.45
  333.8 16.1 %reduce-scatter.2.cloned.1.call-done = f32[256,8]{0,1:T(8,128)} async-done(((f32[1024,8]{0,1:T(8,128)}), f32[256,8]{0,1:T(8,128)}) %reduce-scatter.2.cloned.1.call-update) | async-done | bytes 8208 | tf_op jit(solution)/shard_map/reduce_scatter | solution.py:237
  349.9 0.7 fusion.89
  350.6 41.0 %all_gather.3 = bf16[8,8192]{1,0:T(8,128)(2,1)S(1)} all-gather(bf16[8,256]{1,0:T(8,128)(2,1)S(1)} %fusion.89), channel_id=1, replica_groups=mesh['seq'=8,'chan'=4] {'seq','chan'}, dimensions={1}, use_global_device_ids=true | all-gather | bytes 135168 | tf_op jit(solution)/shard_map/all_gather | solution.py:245
  391.9 8.2 %convolution_convert_fusion = bf16[8,1024]{1,0:T(8,128)(2,1)S(1)} fusion(bf16[8192,1024]{1,0:T(8,128)(2,1)} %bitcast.147, bf16[8,8192]{1,0:T(8,128)(2,1)S(1)} %all_gather.3, f32[8192]{0:T(1024)S(1)} %bitcast.151, f32[8]{0:T(128)S(1)} %add_rsqrt_fusion), kind=kOutput, calls=%fused_computation.37 | convolution fusion | flops 134488064 | bytes 16957472 | tf_op jit(solution)/shard_map/dot_general | solution.py:30
  400.2 0.2 fusion.19
  400.5 37.0 %psum.54 = f32[8,544]{1,0:T(8,128)S(1)} all-reduce(f32[8,544]{1,0:T(8,128)S(1)} %fusion.19), channel_id=1, replica_groups=mesh['seq'=8,'chan'=4] {'seq','chan'}, use_global_device_ids=true, to_apply=%region_25.26 | all-reduce | flops 4352 | bytes 34816 | tf_op jit(solution)/shard_map/psum | solution.py:44
  437.5 0.2 fusion.111
  438.0 5.3 fusion.9
  443.4 0.6 pad_maximum_fusion.1
  444.0 0.8 pad_maximum_fusion
  444.8 125.8 %all-reduce.6.cloned.1.call-done = f32[8,8192]{1,0:T(8,128)} async-done(((f32[8,8192]{1,0:T(8,128)}), f32[8,8192]{1,0:T(8,128)}) %all-reduce.6.cloned.1.call-update) | async-done | bytes 262160 | tf_op jit(solution)/shard_map/psum | solution.py:64
  570.6 1.3 add_convert_fusion
  (110 shorter events, 2.4 us)
Async XLA Ops:
  7.2 83.1 %copy-start = (s32[8]{0:T(128)S(1)}, s32[8]{0:T(128)}, u32[]{:S(2)}) copy-start(s32[8]{0:T(128)} %param.36) | copy-start | bytes 100
  7.2 209.4 %all-reduce.4.cloned.1.call-start = ((), (), s32[]{:S(2)}) async-start(), calls=%async_computation.1 | async-start | bytes 524288 | tf_op jit(solution)/shard_map/psum | solution.py:64
  33.1 3.1 copy-start.13
  33.1 3.7 copy-start.2
  37.0 2.4 copy-start.16
  37.0 2.5 copy-start.19
  37.0 3.1 copy-start.23
  37.1 3.7 copy-start.3
  37.1 46.1 %copy-start.24 = (f32[2,512]{1,0:T(2,128)S(1)}, f32[2,512]{1,0:T(2,128)}, u32[]{:S(2)}) copy-start(f32[2,512]{1,0:T(2,128)} %param.28) | copy-start | bytes 12292
  37.1 46.6 %copy-start.15 = (f32[2,16,512]{2,1,0:T(8,128)S(1)}, f32[2,16,512]{2,1,0:T(8,128)}, u32[]{:S(2)}) copy-start(f32[2,16,512]{2,1,0:T(8,128)} %param.29) | copy-start | bytes 196612
  37.1 46.7 %copy-start.25 = (f32[2,512]{1,0:T(2,128)S(1)}, f32[2,512]{1,0:T(2,128)}, u32[]{:S(2)}) copy-start(f32[2,512]{1,0:T(2,128)} %param.30) | copy-start | bytes 12292
  37.1 47.2 %copy-start.5 = (bf16[2,512,512]{2,1,0:T(8,128)(2,1)S(1)}, bf16[2,512,512]{2,1,0:T(8,128)(2,1)}, u32[]{:S(2)}) copy-start(bf16[2,512,512]{2,1,0:T(8,128)(2,1)} %param.27) | copy-start | bytes 3145732
  37.1 47.4 %copy-start.1 = (f32[2,8,16,512]{3,2,1,0:T(8,128)S(1)}, f32[2,8,16,512]{3,2,1,0:T(8,128)}, u32[]{:S(2)}) copy-start(f32[2,8,16,512]{3,2,1,0:T(8,128)} %param.31) | copy-start | bytes 1572868
  39.4 50.6 %copy-start.18 = (s32[8,8]{1,0:T(8,128)S(1)}, s32[8,8]{1,0:T(8,128)}, u32[]{:S(2)}) copy-start(s32[8,8]{1,0:T(8,128)} %param.37) | copy-start | bytes 772
  39.5 44.8 %copy-start.11 = (bf16[8,1,512]{2,0,1:T(8,128)(2,1)}, bf16[8,1,512]{2,0,1:T(8,128)(2,1)S(1)}, u32[]{:S(2)}) copy-start(bf16[8,1,512]{2,0,1:T(8,128)(2,1)S(1)} %slice_bitcast_fusion.9) | copy-start | bytes 24580
  39.5 76.0 %copy-start.7 = (bf16[8,3,512]{2,0,1:T(8,128)(2,1)}, bf16[8,3,512]{2,0,1:T(8,128)(2,1)S(1)}, u32[]{:S(2)}) copy-start(bf16[8,3,512]{2,0,1:T(8,128)(2,1)S(1)} %get-tuple-element.151) | copy-start | bytes 73732
  84.5 31.0 %copy-start.9 = (f32[8,512]{1,0:T(8,128)}, f32[8,512]{1,0:T(8,128)S(1)}, u32[]{:S(2)}) copy-start(f32[8,512]{1,0:T(8,128)S(1)} %get-tuple-element.161) | copy-start | bytes 49156
  90.0 259.9 %reduce-scatter.2.cloned.1.call-start = ((), (), s32[]{:S(2)}) async-start(), calls=%async_computation.2 | async-start | bytes 40960 | tf_op jit(solution)/shard_map/reduce_scatter | solution.py:237
  221.1 111.4 %copy-start.8 = (bf16[8,3,512]{2,0,1:T(8,128)(2,1)S(1)}, bf16[8,3,512]{2,0,1:T(8,128)(2,1)}, u32[]{:S(2)}) copy-start(bf16[8,3,512]{2,0,1:T(8,128)(2,1)} %copy-done.7) | copy-start | bytes 73732
  258.4 74.1 %copy-start.12 = (bf16[8,1,512]{2,0,1:T(8,128)(2,1)S(1)}, bf16[8,1,512]{2,0,1:T(8,128)(2,1)}, u32[]{:S(2)}) copy-start(bf16[8,1,512]{2,0,1:T(8,128)(2,1)} %copy-done.11) | copy-start | bytes 24580
  258.4 74.0 %copy-start.14 = (bf16[8,2,2,128]{3,0,2,1:T(8,128)(2,1)}, bf16[8,2,2,128]{3,0,2,1:T(8,128)(2,1)S(1)}, u32[]{:S(2)}) copy-start(bf16[8,2,2,128]{3,0,2,1:T(8,128)(2,1)S(1)} %slice_bitcast_fusion.8) | copy-start | bytes 24580
  332.4 238.2 %all-reduce.6.cloned.1.call-start = ((), (), s32[]{:S(2)}) async-start(), calls=%async_computation.3 | async-start | bytes 524288 | tf_op jit(solution)/shard_map/psum | solution.py:64
  391.8 8.3 %copy-start.17 = (f32[4,512]{1,0:T(4,128)S(1)}, f32[4,512]{1,0:T(4,128)}, u32[]{:S(2)}) copy-start(f32[4,512]{1,0:T(4,128)} %get-tuple-element.158) | copy-start | bytes 24580
  391.8 8.3 %copy-start.22 = (f32[1,512]{1,0:T(1,128)S(1)}, f32[1,512]{1,0:T(1,128)}, u32[]{:S(2)}) copy-start(f32[1,512]{1,0:T(1,128)} %get-tuple-element.168) | copy-start | bytes 6148
  391.9 8.4 %copy-start.4 = (bf16[2,512,544]{1,2,0:T(8,128)(2,1)S(1)}, bf16[2,512,544]{1,2,0:T(8,128)(2,1)}, u32[]{:S(2)}) copy-start(bf16[2,512,544]{1,2,0:T(8,128)(2,1)} %param.26) | copy-start | bytes 3342340
  391.9 45.7 %copy-start.6 = (bf16[2,512,512]{2,1,0:T(8,128)(2,1)S(1)}, bf16[2,512,512]{2,1,0:T(8,128)(2,1)}, u32[]{:S(2)}) copy-start(bf16[2,512,512]{2,1,0:T(8,128)(2,1)} %param.27) | copy-start | bytes 3145732
  391.9 45.6 %copy-start.21 = (f32[1,512]{1,0:T(1,128)S(1)}, f32[1,512]{1,0:T(1,128)}, u32[]{:S(2)}) copy-start(f32[1,512]{1,0:T(1,128)} %get-tuple-element.166) | copy-start | bytes 6148
  391.9 45.8 %copy-start.10 = (f32[8,512]{1,0:T(8,128)S(1)}, f32[8,512]{1,0:T(8,128)}, u32[]{:S(2)}) copy-start(f32[8,512]{1,0:T(8,128)} %copy-done.9) | copy-start | bytes 49156
  391.9 46.1 %copy-start.20 = (f32[1,512]{1,0:T(1,128)S(1)}, f32[1,512]{1,0:T(1,128)}, u32[]{:S(2)}) copy-start(f32[1,512]{1,0:T(1,128)} %get-tuple-element.164) | copy-start | bytes 6148
Sparse Core Ops, SparseCore 0:
  90.1 126.4 all-reduce.3
  332.5 17.3 reduce-scatter.1
  443.5 127.0 all-reduce.5
where the time goes:
time: 579 us; the launch traced here: 578 us
  waiting for transfers between devices  240 us (41%)
  blocking collectives  216 us (37%)
  local copies, waits for them, and re-layouts  61.4 us (11%)
  matrix products  31 us (5%)
  between operations  15 us (3%)
  other arithmetic  14.6 us (3%)
    psum x2, waiting for transfers between devices, mix_out(): lax.psum(jnp.dot(gated_out, weights_now, preferred_element_type=jnp.float...  224 us
    psum x2, blocking collectives, mamba_mix(): mapped_vectors = lax.psum(x_terms, ('seq', 'chan'))  79.1 us
    all_gather x1, blocking collectives, shards(): lax.all_gather(stream_two, ('seq', 'chan'), axis=1, tiled=True)  41 us
    psum x1, blocking collectives, attend(): lax.psum(qkv_terms, 'seq').astype(jnp.bfloat16)  37.3 us
    psum x1, blocking collectives, attend(): lax.psum((local_acc * rescale[..., None]).astype(jnp.bfloat16), 'seq')  33.4 us
    slice x1, local copies, waits for them, and re-layouts, mamba_mix(): in_weight[layer].reshape(in_weight.shape[1], 2 * channels)  25.8 us
    pmax x1, blocking collectives, attend(): grand_top = lax.pmax(local_top, 'seq')  25.2 us
    unnamed x55, local copies, waits for them, and re-layouts  21.1 us
  transfers between devices with their start and end apart: 3, of which 3 were waited for; matrix products, arithmetic and copies ran while one was open for 5% of the time, Pallas kernels for 0%

commit v1 on v0

--- a/solution.py
+++ b/solution.py
@@ -1,10 +1,250 @@
+import functools
+
 import jax
 import jax.numpy as jnp
 from jax import lax
+from jax.experimental import pallas as pl
+from jax.experimental.pallas import tpu as pltpu
 from jax.sharding import PartitionSpec as P
 
 norm_eps = 1e-06
 lowest_score = -1e30
+wire = jnp.bfloat16
+
+
+def greet(sizes):
+    barrier = pltpu.get_barrier_semaphore()
+    count = 0
+    for axis, size in sizes:
+        me = lax.axis_index(axis)
+        for hop in range(1, size):
+            pl.semaphore_signal(
+                barrier,
+                inc=1,
+                device_id={axis: lax.rem(me + hop, size)},
+                device_id_type=pl.DeviceIdType.MESH,
+            )
+            count += 1
+    pl.semaphore_wait(barrier, count)
+
+
+def send_all(axis, size, source, target, send_sems, recv_sems):
+    me = lax.axis_index(axis)
+    copies = []
+    for hop in range(1, size):
+        peer = lax.rem(me + hop, size)
+        copy = pltpu.make_async_remote_copy(
+            src_ref=source(peer),
+            dst_ref=target(hop),
+            send_sem=send_sems.at[hop],
+            recv_sem=recv_sems.at[hop],
+            device_id={axis: peer},
+            device_id_type=pl.DeviceIdType.MESH,
+        )
+        copy.start()
+        copies.append(copy)
+    return copies
+
+
+def wait_all(copies):
+    for copy in copies:
+        copy.wait()
+
+
+def summed(own, landed, size):
+    total = own.astype(jnp.float32)
+    for hop in range(1, size):
+        total = total + landed[hop].astype(jnp.float32)
+    return total
+
+
+def sems(size):
+    return [pltpu.SemaphoreType.DMA((size,)), pltpu.SemaphoreType.DMA((size,))]
+
+
+def comm_call(kernel, outs, scratch, collective_id, *operands):
+    vmem = pl.BlockSpec(memory_space=pltpu.VMEM)
+    return pl.pallas_call(
+        kernel,
+        out_shape=outs,
+        in_specs=[vmem] * len(operands),
+        out_specs=jax.tree.map(lambda _: vmem, outs),
+        scratch_shapes=scratch,
+        compiler_params=pltpu.CompilerParams(
+            collective_id=collective_id, has_side_effects=True, vmem_limit_bytes=4 * 1024 * 1024
+        ),
+        cost_estimate=pl.CostEstimate(flops=0, bytes_accessed=16 * 1024 * 1024, transcendentals=0),
+    )(*operands)
+
+
+def all_sum_kernel(sizes, x_ref, out_ref, land_a, mid, land_b, sa, ra, sb, rb):
+    seq, chan = sizes
+    greet((("seq", seq), ("chan", chan)))
+    wait_all(send_all("chan", chan, lambda p: x_ref, lambda h: land_a.at[h], sa, ra))
+    mid[...] = summed(x_ref[...], land_a, chan).astype(mid.dtype)
+    wait_all(send_all("seq", seq, lambda p: mid, lambda h: land_b.at[h], sb, rb))
+    out_ref[...] = summed(mid[...], land_b, seq)
+
+
+def all_sum(x, collective_id):
+    seq, chan = lax.axis_size("seq"), lax.axis_size("chan")
+    x = x.astype(wire)
+    scratch = [
+        pltpu.VMEM((chan,) + x.shape, wire),
+        pltpu.VMEM(x.shape, wire),
+        pltpu.VMEM((seq,) + x.shape, wire),
+    ]
+    return comm_call(
+        functools.partial(all_sum_kernel, (seq, chan)),
+        jax.ShapeDtypeStruct(x.shape, jnp.float32),
+        scratch + sems(chan) + sems(seq),
+        collective_id,
+        x,
+    )
+
+
+def share_sum_kernel(sizes, spread, x_ref, base_ref, out_ref, *rest):
+    seq, chan = sizes
+    if spread:
+        block_ref, land_a, mid, land_b, sa, ra, sb, rb, sc, rc = rest
+    else:
+        land_a, mid, land_b, sa, ra, sb, rb = rest
+    me_seq, me_chan = lax.axis_index("seq"), lax.axis_index("chan")
+    greet((("seq", seq), ("chan", chan)))
+    wait_all(send_all("chan", chan, lambda p: x_ref.at[p], lambda h: land_a.at[h], sa, ra))
+    mid[...] = summed(x_ref[me_chan], land_a, chan).astype(mid.dtype)
+    wait_all(send_all("seq", seq, lambda p: mid.at[p], lambda h: land_b.at[h], sb, rb))
+    added = summed(mid[me_seq], land_b, seq)
+    result = (base_ref[...].astype(jnp.float32) + added).astype(out_ref.dtype)
+    out_ref[...] = result
+    if spread:
+        block_ref[me_chan] = result
+        wait_all(
+            send_all("chan", chan, lambda p: out_ref, lambda h: block_ref.at[me_chan], sc, rc)
+        )
+
+
+def share_sum(partial, base, spread, collective_id):
+    seq, chan = lax.axis_size("seq"), lax.axis_size("chan")
+    rows, width = base.shape
+    x = partial.astype(wire).reshape(rows, seq, chan, width).transpose(2, 1, 0, 3)
+    outs = [jax.ShapeDtypeStruct(base.shape, jnp.bfloat16)]
+    scratch = [
+        pltpu.VMEM((chan, seq, rows, width), wire),
+        pltpu.VMEM((seq, rows, width), wire),
+        pltpu.VMEM((seq, rows, width), wire),
+    ]
+    scratch = scratch + sems(chan) + sems(seq)
+    if spread:
+        outs.append(jax.ShapeDtypeStruct((chan, rows, width), jnp.bfloat16))
+        scratch = scratch + sems(chan)
+    return comm_call(
+        functools.partial(share_sum_kernel, (seq, chan), spread),
+        outs,
+        scratch,
+        collective_id,
+        x,
+        base,
+    )
+
+
+def seq_sum_kernel(seq, x_ref, square_ref, out_ref, squares_ref, land, mid, sa, ra, sb, rb, sc, rc):
+    me = lax.axis_index("seq")
+    greet((("seq", seq),))
+    first = send_all("seq", seq, lambda p: x_ref.at[p], lambda h: land.at[h], sa, ra)
+    second = send_all("seq", seq, lambda p: square_ref, lambda h: squares_ref.at[h], sb, rb)
+    squares_ref[0] = square_ref[...]
+    wait_all(first)
+    total = summed(x_ref[me], land, seq).astype(mid.dtype)
+    mid[...] = total
+    out_ref[me] = total
+    third = send_all("seq", seq, lambda p: mid, lambda h: out_ref.at[me], sc, rc)
+    wait_all(second)
+    wait_all(third)
+
+
+def seq_sum(x, squares, collective_id):
+    seq = lax.axis_size("seq")
+    lanes = 128
+    flat = x.astype(wire).reshape(-1, lanes)
+    piece = -(-flat.shape[0] // seq)
+    padded = jnp.pad(flat, ((0, piece * seq - flat.shape[0]), (0, 0))).reshape(seq, piece, lanes)
+    spread = jnp.broadcast_to(squares[:, None], (squares.shape[0], lanes))
+    result, gathered = comm_call(
+        functools.partial(seq_sum_kernel, seq),
+        [
+            jax.ShapeDtypeStruct(padded.shape, wire),
+            jax.ShapeDtypeStruct((seq,) + spread.shape, jnp.float32),
+        ],
+        [pltpu.VMEM(padded.shape, wire), pltpu.VMEM(padded.shape[1:], wire)]
+        + sems(seq)
+        + sems(seq)
+        + sems(seq),
+        collective_id,
+        padded,
+        spread,
+    )
+    whole = result.reshape(-1, lanes)[: flat.shape[0]].reshape(x.shape)
+    return whole.astype(jnp.float32), jnp.sum(gathered[:, :, 0], axis=0)
+
+
+def seq_collect_kernel(seq, a_ref, b_ref, a_all, b_all, sa, ra, sb, rb):
+    greet((("seq", seq),))
+    first = send_all("seq", seq, lambda p: b_ref, lambda h: b_all.at[h], sb, rb)
+    second = send_all("seq", seq, lambda p: a_ref, lambda h: a_all.at[h], sa, ra)
+    a_all[0] = a_ref[...]
+    b_all[0] = b_ref[...]
+    wait_all(first)
+    wait_all(second)
+
+
+def seq_collect(a, b, collective_id):
+    seq = lax.axis_size("seq")
+    return comm_call(
+        functools.partial(seq_collect_kernel, seq),
+        [
+            jax.ShapeDtypeStruct((seq,) + a.shape, a.dtype),
+            jax.ShapeDtypeStruct((seq,) + b.shape, b.dtype),
+        ],
+        sems(seq) + sems(seq),
+        collective_id,
+        a,
+        b,
+    )
+
+
+def chan_sum_kernel(sizes, x_ref, base_ref, out_ref, all_ref, land, sa, ra, sb, rb, sc, rc):
+    seq, chan = sizes
+    me_seq, me_chan = lax.axis_index("seq"), lax.axis_index("chan")
+    greet((("seq", seq), ("chan", chan)))
+    wait_all(send_all("chan", chan, lambda p: x_ref.at[p], lambda h: land.at[h], sa, ra))
+    added = summed(x_ref[me_chan], land, chan)
+    result = (base_ref[...].astype(jnp.float32) + added).astype(out_ref.dtype)
+    out_ref[...] = result
+    all_ref[me_seq, me_chan] = result
+    wait_all(
+        send_all("chan", chan, lambda p: out_ref, lambda h: all_ref.at[me_seq, me_chan], sb, rb)
+    )
+    mine = all_ref.at[me_seq]
+    wait_all(send_all("seq", seq, lambda p: mine, lambda h: all_ref.at[me_seq], sc, rc))
+
+
+def chan_sum(partial, base, collective_id):
+    seq, chan = lax.axis_size("seq"), lax.axis_size("chan")
+    rows, width = base.shape
+    x = partial.astype(wire).reshape(rows, chan, width).transpose(1, 0, 2)
+    share, every = comm_call(
+        functools.partial(chan_sum_kernel, (seq, chan)),
+        [
+            jax.ShapeDtypeStruct(base.shape, jnp.bfloat16),
+            jax.ShapeDtypeStruct((seq, chan, rows, width), jnp.bfloat16),
+        ],
+        [pltpu.VMEM(x.shape, wire)] + sems(chan) + sems(chan) + sems(seq),
+        collective_id,
+        x,
+        base,
+    )
+    return share, every.transpose(2, 0, 1, 3).reshape(rows, seq * chan * width)
 
 
 def normalize(stream, gain_row):
@@ -41,7 +281,7 @@
     )
     signal = lax.optimization_barrier(jax.nn.silu(conv_sum).astype(jnp.bfloat16))
     x_terms = jnp.dot(signal, xproj_weight[layer], preferred_element_type=jnp.float32)
-    mapped_vectors = lax.psum(x_terms, ("seq", "chan"))
+    mapped_vectors = all_sum(x_terms, 10 + layer)
     low_rank = dt_weight.shape[1]
     state_size = a_log.shape[1]
     dt_low = mapped_vectors[:, :low_rank].astype(jnp.bfloat16)
@@ -59,24 +299,18 @@
     return (gated_out, fresh_state, window[:, 1:, :])
 
 
-def mix_out(gated_out, out_weight, layer):
-    weights_now = out_weight[layer]
-    summed = lax.psum(
-        jnp.dot(gated_out, weights_now, preferred_element_type=jnp.float32), ("seq", "chan")
-    )
-    return summed
-
-
-def attend(normed, asker_lookup_matrix, kv_cache, lengths, page_table):
-    requests = normed.shape[0]
+def attend(scaled, squares, model_dim, asker_lookup_matrix, kv_cache, lengths, page_table):
+    requests = scaled.shape[0]
     heads_kv = asker_lookup_matrix.shape[1]
     per_lens_width = kv_cache.shape[4]
     group_size = asker_lookup_matrix.shape[2] // per_lens_width - 2
     inv_sqrt = per_lens_width ** (-0.5)
     qkv_terms = jnp.einsum(
-        "bd,dkc->bkc", normed, asker_lookup_matrix, preferred_element_type=jnp.float32
-    )
-    qkv_all = lax.optimization_barrier(lax.psum(qkv_terms, "seq").astype(jnp.bfloat16))
+        "bd,dkc->bkc", scaled, asker_lookup_matrix, preferred_element_type=jnp.float32
+    )
+    qkv_sum, square_sum = seq_sum(qkv_terms, squares, 12)
+    inv_rms = lax.rsqrt(square_sum / model_dim + norm_eps)
+    qkv_all = lax.optimization_barrier((qkv_sum * inv_rms[:, None, None]).astype(jnp.bfloat16))
     every_question = qkv_all[:, :, : group_size * per_lens_width].reshape(
         requests, heads_kv, group_size, per_lens_width
     )
@@ -159,12 +393,18 @@
     factor = jnp.where(chosen, jnp.exp(page_tops[None] - local_top[:, None]), 0.0)
     local_sum = jnp.sum(factor * page_sums[None], axis=1)
     local_acc = jnp.einsum("bpkg,pkgd->bkgd", factor, page_accs, precision=lax.Precision.HIGHEST)
-    grand_top = lax.pmax(local_top, "seq")
-    rescale = jnp.exp(local_top - grand_top)
-    weight_total, value_total = (
-        lax.psum((local_sum * rescale).astype(jnp.bfloat16), "seq").astype(jnp.float32),
-        lax.psum((local_acc * rescale[..., None]).astype(jnp.bfloat16), "seq").astype(jnp.float32),
-    )
+    packed = jnp.stack([local_top, local_sum]).reshape(2, -1)
+    accs_all, packed_all = seq_collect(
+        local_acc.astype(wire).reshape(-1, per_lens_width), packed, 13
+    )
+    seq = accs_all.shape[0]
+    tops = packed_all[:, 0].reshape((seq,) + local_top.shape)
+    sums = packed_all[:, 1].reshape((seq,) + local_top.shape)
+    accs = accs_all.reshape((seq,) + local_acc.shape).astype(jnp.float32)
+    grand_top = jnp.max(tops, axis=0)
+    rescale = jnp.exp(tops - grand_top[None])
+    weight_total = jnp.sum(sums * rescale, axis=0)
+    value_total = jnp.sum(accs * rescale[..., None], axis=0)
     fresh_score = (
         jnp.einsum(
             "ujqf,ujf->ujq",
@@ -224,31 +464,22 @@
     share_index = seq_index * lax.axis_size("chan") + lax.axis_index("chan")
     normed = normalize(hidden, norm_gain[0])
     gated_first, state_first, conv_first = mamba_mix(normed, 0, layer_params)
-    stream_full = (hidden.astype(jnp.float32) + mix_out(gated_first, out_weight, 0)).astype(
-        jnp.bfloat16
-    )
-    stream_one = lax.dynamic_slice_in_dim(stream_full, share_index * share_cols, share_cols, 1)
-    widened = stream_full.astype(jnp.float32)
-    inv_rms = lax.rsqrt(jnp.mean(widened * widened, axis=1) + norm_eps)
-    block_rows = lax.dynamic_slice_in_dim(widened, seq_index * block_cols, block_cols, 1)
+    first_terms = jnp.dot(gated_first, out_weight[0], preferred_element_type=jnp.float32)
+    hidden_share = lax.dynamic_slice_in_dim(hidden, share_index * share_cols, share_cols, 1)
+    stream_one, block = share_sum(first_terms, hidden_share, True, 14)
+    widened = block.transpose(1, 0, 2).reshape(hidden.shape[0], block_cols).astype(jnp.float32)
     gain_block = lax.dynamic_slice_in_dim(norm_gain[1], seq_index * block_cols, block_cols, 0)
-    attn_in = (block_rows * inv_rms[:, None] * gain_block[None, :]).astype(jnp.bfloat16)
-    attended, newest_pair = attend(attn_in, asker_lookup_matrix, kv_cache, lengths, page_table)
-    attn_share = lax.psum_scatter(
-        jnp.einsum("khc,bkh->cb", o_weight, attended, preferred_element_type=jnp.float32),
-        "chan",
-        scatter_dimension=0,
-        tiled=True,
-    )
-    stream_two = (stream_one.astype(jnp.float32) + attn_share.T).astype(jnp.bfloat16)
-    normed_two = normalize(
-        lax.all_gather(stream_two, ("seq", "chan"), axis=1, tiled=True), norm_gain[2]
-    )
+    scaled = (widened * gain_block[None, :]).astype(jnp.bfloat16)
+    squares = jnp.sum(widened * widened, axis=1)
+    attended, newest_pair = attend(
+        scaled, squares, model_dim, asker_lookup_matrix, kv_cache, lengths, page_table
+    )
+    attn_terms = jnp.einsum("khc,bkh->bc", o_weight, attended, preferred_element_type=jnp.float32)
+    stream_two, every = chan_sum(attn_terms, stream_one, 15)
+    normed_two = normalize(every, norm_gain[2])
     gated_two, state_two, conv_two = mamba_mix(normed_two, 1, layer_params)
-    added = lax.dynamic_slice_in_dim(
-        mix_out(gated_two, out_weight, 1), share_index * share_cols, share_cols, 1
-    )
-    hidden_out = (stream_two.astype(jnp.float32) + added).astype(jnp.bfloat16)
+    last_terms = jnp.dot(gated_two, out_weight[1], preferred_element_type=jnp.float32)
+    (hidden_out,) = share_sum(last_terms, stream_two, False, 16)
     return (
         hidden_out,
         jnp.stack([state_first, state_two]),

time: 579 us -> 164 us (0.28)
  waiting for transfers between devices: 240 us -> 0 us
  blocking collectives: 216 us -> 0 us
  Pallas kernels: 0 us -> 83 us
  local copies, waits for them, and re-layouts: 61.4 us -> 48.3 us
  between operations: 15 us -> 2.09 us
  matrix products: 31 us -> 21.6 us
  other arithmetic: 14.6 us -> 8.4 us
    psum x2 -> x0, waiting for transfers between devices: 224 us -> none  [mix_out(): lax.psum(jnp.dot(gated_out, weights_now, preferred_element_type=jnp.float...]
    psum x4 -> x0, blocking collectives: 150 us -> none  [the longest x2 79.1 us: mamba_mix(): mapped_vectors = lax.psum(x_terms, ('seq', 'chan'))]
    pallas_call x0 -> x7, Pallas kernels: none -> 83 us  [comm_call(): pl.pallas_call(kernel, out_shape=outs, in_specs=[vmem] * len(operands), o...]
    all_gather x1 -> x0, blocking collectives: 41 us -> none  [shards(): lax.all_gather(stream_two, ('seq', 'chan'), axis=1, tiled=True)]
    pmax x1 -> x0, blocking collectives: 25.2 us -> none  [attend(): grand_top = lax.pmax(local_top, 'seq')]
    reduce_scatter x1 -> x0, waiting for transfers between devices: 16.1 us -> none  [shards(): lax.psum_scatter(jnp.einsum('khc,bkh->cb', o_weight, attended, preferred_...]
    unnamed x55 -> x36, local copies, waits for them, and re-layouts: 21.1 us -> 15.1 us
    dot_general x2, matrix products: 10.5 us -> 4.57 us  [mamba_mix(): jnp.dot(normed, in_weight[layer].reshape(in_weight.shape[1], 2 * channels...]
  transfers between devices with their start and end apart: 3 -> 0, of which waited for: 3 -> 0; matrix products, arithmetic and copies ran while one was open for 5% -> 0% of each run, Pallas kernels for 0% -> 0%
where the time goes in v1:
time: 164 us
  Pallas kernels  83 us (51%)
  local copies, waits for them, and re-layouts  48.3 us (29%)
  matrix products  21.6 us (13%)
  other arithmetic  8.4 us (5%)
  between operations  2.09 us (1%)
    pallas_call x7, Pallas kernels, comm_call(): pl.pallas_call(kernel, out_shape=outs, in_specs=[vmem] * len(operands), o...  83 us
    slice x1, local copies, waits for them, and re-layouts, mamba_mix(): in_weight[layer].reshape(in_weight.shape[1], 2 * channels)  25.8 us
    unnamed x36, local copies, waits for them, and re-layouts  15.1 us
    dot_general x1, matrix products, shards(): jnp.dot(gated_two, out_weight[1], preferred_element_type=jnp.float32)  4.58 us
    dot_general x1, matrix products, shards(): jnp.dot(gated_first, out_weight[0], preferred_element_type=jnp.float32)  4.58 us
    dot_general x2, matrix products, mamba_mix(): jnp.dot(normed, in_weight[layer].reshape(in_weight.shape[1], 2 * channels...  4.57 us
    dot_general x1, matrix products, attend(): jnp.einsum('bd,dkc->bkc', scaled, asker_lookup_matrix, preferred_element_...  3.28 us

profile of v1, /device:TPU:0, one launch (start us, length us, event | category | flops | bytes accessed | tf_op | source)
XLA Modules:
  0.0 163.7 jit_solution(5816252750797127546)
XLA Ops:
  0.7 0.8 compare_reduce_fusion
  1.5 0.6 gather_fusion.2
  2.1 0.8 fusion.44
  2.9 0.6 iota_add_fusion
  4.2 1.0 sort.17
  5.2 0.6 gather_fusion.3
  5.9 0.7 broadcast_select_fusion
  6.5 0.6 gather_fusion.4
  7.2 25.8 %fusion.93 = (bf16[1,8192,2,512]{3,2,1,0:T(2,128)(2,1)}, bf16[1,8192,2,512]{3,2,1,0:T(2,128)(2,1)S(1)}) fusion(bf16[2,8192,2,512]{3,2,1,0:T(2,128)(2,1)} %param.22), kind=kLoop, calls=%fused_computation.189 | loop fusion | bytes 67108864 | tf_op jit(solution)/shard_map/slice | solution.py:272
  33.0 3.0 %copy.95 = bf16[1024,8,2,512]{3,1,2,0:T(8,128)(2,1)S(1)} copy(bf16[1024,8,2,512]{3,2,1,0:T(2,128)(2,1)S(1)} %bitcast.153) | data formatting | bytes 33554432
  36.1 0.1 slice_reduce_fusion
  36.2 0.2 fusion.28
  36.5 2.3 %convolution_convert_fusion.4 = bf16[8,1024]{1,0:T(8,128)(2,1)S(1)} fusion(bf16[8192,1024]{1,0:T(8,128)(2,1)S(1)} %bitcast.150, bf16[8,8192]{1,0:T(8,128)(2,1)S(1)} %copy-done.7, f32[8192]{0:T(1024)S(1)} %bitcast.155, f32[8]{0:T(128)S(1)} %add_rsqrt_fusion.2), kind=kOutput, calls=%fused_computation.39 | convolution fusion | flops 134488064 | bytes 16957472 | tf_op jit(solution)/shard_map/dot_general | solution.py:270
  38.9 0.2 convolution_convert_fusion.6.x_ref
  39.2 12.2 %shard_map.201 = f32[8,544]{1,0:T(8,128)S(1)} custom-call(bf16[8,544]{1,0:T(8,128)(2,1)S(1)} %convolution_convert_fusion.6.x_ref), custom_call_target="tpu_custom_call" | custom-call | bytes 16777216 | tf_op jit(solution)/shard_map/pallas_call | solution.py:67
  51.5 0.2 fusion.97
  51.7 0.1 fusion.39
  51.9 4.6 %convolution_convert_fusion.1 = bf16[8,8192]{1,0:T(8,128)(2,1)S(1)} fusion(bf16[2,512,8192]{2,1,0:T(8,128)(2,1)} %param.32, f32[8,512]{1,0:T(8,128)S(1)} %fusion.39, bf16[8,512]{1,0:T(8,128)(2,1)S(1)} %multiply_convert_fusion.3, bf16[8,1024]{1,0:T(8,128)(2,1)S(1)} %convolution_convert_fusion.4, f32[512]{0:T(512)S(1)} %bitcast.163), kind=kOutput, calls=%fused_computation.26 | convolution fusion | flops 67215360 | bytes 8554496 | tf_op jit(solution)/shard_map/dot_general | solution.py:467
  56.5 0.1 reshape.206
  56.7 12.5 %shard_map.202 = (bf16[8,256]{1,0:T(8,128)(2,1)S(1)}, bf16[4,8,256]{2,1,0:T(8,128)(2,1)S(1)}) custom-call(bf16[4,8,8,256]{3,2,1,0:T(8,128)(2,1)S(1)} %bitcast.146, bf16[8,256]{1,0:T(8,128)(2,1)S(1)} %constant_dynamic-slice_fusion.base_ref), custom_call_target="tpu_custom_call" | custom-call | bytes 16777216 | tf_op jit(solution)/shard_map/pallas_call | solution.py:67
  69.2 3.3 %fusion.15 = bf16[8,2,1280]{2,0,1:T(8,128)(2,1)S(1)} fusion(bf16[1024,2,1280]{2,1,0:T(2,128)(2,1)} %param.33, f32[8,1024]{1,0:T(8,128)S(1)} %bitcast.156, f32[1024]{0:T(1024)S(1)} %bitcast.159), kind=kOutput, calls=%fused_computation.33 | convolution fusion | flops 41979904 | bytes 5320704 | tf_op jit(solution)/shard_map/bd,dkc->bkc/dot_general | solution.py:308
  72.6 0.1 multiply_reduce_fusion.4
  72.7 12.9 %shard_map.203 = (bf16[8,20,128]{2,1,0:T(8,128)(2,1)S(1)}, f32[8,8,128]{2,1,0:T(8,128)S(1)}) custom-call(bf16[8,20,128]{2,1,0:T(8,128)(2,1)S(1)} %reshape.207.x_ref, f32[8,128]{1,0:T(8,128)S(1)} %broadcast_in_dim.166.square_ref), custom_call_target="tpu_custom_call" | custom-call | bytes 16777216 | tf_op jit(solution)/shard_map/pallas_call | solution.py:67
  85.7 0.1 slice_reduce_fusion.1
  85.8 0.1 multiply_convert_fusion
  86.0 2.1 %copy.67 = bf16[8,256,2,2,128]{4,1,3,2,0:T(8,128)(2,1)S(1)} copy(bf16[8,256,2,2,128]{4,3,2,1,0:T(2,128)(2,1)} %param.35) | data formatting | bytes 4194304 | tf_op jit(solution)/shard_map/while | solution.py:387
  88.1 2.4 %while.14 = (s32[]{:T(128)}, f32[8,2,8]{2,1,0:T(2,128)S(1)}, f32[8,2,8]{2,1,0:T(2,128)S(1)}, f32[8,2,8,128]{3,0,2,1:T(8,128)S(1)}, s32[]{:T(128)}, /*index=5*/s3...) while((s32[]{:T(128)}, f32[8,2,8]{2,1,0:T(2,128)S(1)}, ...), condition=%wide.region_14.15_spmd, body=%wide.region_11.14_spmd.sunk | while | flops 4270546 | bytes 1767079 | solution.py:387
  88.2 0.1 compare_select_fusion.8
  88.3 0.6 gather_fusion
  88.8 0.6 gather_fusion.1
  89.5 0.1 dynamic_slice.24
  89.6 0.2 fusion.118
  89.9 0.2 fusion.119
  90.1 0.2 fusion.120
  90.6 0.7 iota_compare_fusion.2
  91.3 0.1 select_reduce_fusion
  91.4 0.3 fusion.18
  91.8 0.2 multiply_reduce_fusion.2
  92.0 0.1 stack.24
  92.2 0.1 stack.23
  92.3 12.9 %shard_map.204 = (bf16[8,128,128]{2,1,0:T(8,128)(2,1)S(1)}, f32[8,2,128]{2,1,0:T(2,128)S(1)}) custom-call(bf16[128,128]{1,0:T(8,128)(2,1)S(1)} %bitcast.148, f32[2,128]{1,0:T(2,128)S(1)} %pad_maximum_fusion.4.b_ref), custom_call_target="tpu_custom_call" | custom-call | bytes 16777216 | tf_op jit(solution)/shard_map/pallas_call | solution.py:67
  105.3 0.1 reduce_sum.154
  105.4 0.1 sub.64
  105.6 0.1 fusion.83
  105.9 0.1 broadcast_multiply_fusion
  106.0 0.2 multiply_reduce_fusion
  106.5 2.8 %fusion.19 = bf16[8,1024]{1,0:T(8,128)(2,1)S(1)} fusion(bf16[2,1024,1024]{2,1,0:T(8,128)(2,1)} %param.34, bf16[8,2,1024]{2,1,0:T(2,128)(2,1)S(1)} %fusion.43), kind=kOutput, calls=%fused_computation.37 | convolution fusion | flops 33562624 | bytes 4243456 | tf_op jit(solution)/shard_map/khc,bkh->bc/dot_general | solution.py:477
  109.3 12.8 %shard_map.205 = (bf16[8,256]{1,0:T(8,128)(2,1)S(1)}, bf16[8,4,8,256]{3,2,1,0:T(8,128)(2,1)S(1)}) custom-call(bf16[4,8,256]{2,1,0:T(8,128)(2,1)S(1)} %bitcast.149, bf16[8,256]{1,0:T(8,128)(2,1)S(1)} %get-tuple-element.77.base_ref), custom_call_target="tpu_custom_call" | custom-call | bytes 16777216 | tf_op jit(solution)/shard_map/pallas_call | solution.py:67
  122.2 0.2 fusion.31
  122.4 0.1 fusion.33
  122.5 11.4 %copy.96 = bf16[1024,8,2,512]{3,1,2,0:T(8,128)(2,1)S(1)} copy(bf16[1024,8,2,512]{3,2,1,0:T(2,128)(2,1)} %bitcast.152) | data formatting | bytes 33554432
  133.9 2.3 %convolution_convert_fusion.3 = bf16[8,1024]{1,0:T(8,128)(2,1)S(1)} fusion(bf16[8,8192]{1,0:T(8,128)(2,1)S(1)} %bitcast.154, bf16[8192,1024]{1,0:T(8,128)(2,1)S(1)} %bitcast.151), kind=kOutput, calls=%fused_computation.38 | convolution fusion | flops 134225920 | bytes 16924672 | tf_op jit(solution)/shard_map/dot_general | solution.py:270
  136.3 0.2 convolution_convert_fusion.5.x_ref
  136.5 9.9 %shard_map.206 = f32[8,544]{1,0:T(8,128)S(1)} custom-call(bf16[8,544]{1,0:T(8,128)(2,1)S(1)} %convolution_convert_fusion.5.x_ref), custom_call_target="tpu_custom_call" | custom-call | bytes 16777216 | tf_op jit(solution)/shard_map/pallas_call | solution.py:67
  146.5 0.2 fusion.96
  146.7 0.1 fusion.36
  146.8 4.6 %convolution_convert_fusion = bf16[8,8192]{1,0:T(8,128)(2,1)S(1)} fusion(bf16[2,512,8192]{2,1,0:T(8,128)(2,1)} %param.32, f32[8,512]{1,0:T(8,128)S(1)} %fusion.36, bf16[8,512]{1,0:T(8,128)(2,1)S(1)} %multiply_convert_fusion.2, bf16[8,1024]{1,0:T(8,128)(2,1)S(1)} %convolution_convert_fusion.3, f32[512]{0:T(512)S(1)} %bitcast.161), kind=kOutput, calls=%fused_computation.25 | convolution fusion | flops 67215360 | bytes 8554496 | tf_op jit(solution)/shard_map/dot_general | solution.py:481
  151.4 0.1 reshape.212
  151.5 0.1 copy.109
  151.6 9.9 %shard_map.207 = bf16[8,256]{1,0:T(8,128)(2,1)S(1)} custom-call(bf16[4,8,8,256]{3,2,1,0:T(8,128)(2,1)S(1)} %bitcast.147, bf16[8,256]{1,0:T(8,128)(2,1)S(1)} %get-tuple-element.79.base_ref), custom_call_target="tpu_custom_call" | custom-call | bytes 16777216 | tf_op jit(solution)/shard_map/pallas_call | solution.py:67
  161.4 0.2 multiply_add_fusion.1
  161.6 0.8 pad_maximum_fusion
  162.4 0.6 pad_maximum_fusion.1
  163.1 0.6 copy.130
  (99 shorter events, 1.8 us)
Async XLA Ops:
  0.6 0.9 copy-start
  33.0 3.1 %copy-start.8 = (f32[3,8192]{1,0:T(4,128)S(1)}, f32[3,8192]{1,0:T(4,128)}, u32[]{:S(2)}) copy-start(f32[3,8192]{1,0:T(4,128)} %param.21) | copy-start | bytes 294916
  33.0 3.2 %copy-start.7 = (bf16[8,8192]{1,0:T(8,128)(2,1)S(1)}, bf16[8,8192]{1,0:T(8,128)(2,1)}, u32[]{:S(2)}) copy-start(bf16[8,8192]{1,0:T(8,128)(2,1)} %param.20) | copy-start | bytes 393220
  36.4 2.4 %copy-start.11 = (bf16[2,8,3,512]{3,1,2,0:T(8,128)(2,1)S(1)}, bf16[2,8,3,512]{3,1,2,0:T(8,128)(2,1)}, u32[]{:S(2)}) copy-start(bf16[2,8,3,512]{3,1,2,0:T(8,128)(2,1)} %param.25) | copy-start | bytes 147460
  36.4 2.4 %copy-start.12 = (f32[2,4,512]{2,1,0:T(4,128)S(1)}, f32[2,4,512]{2,1,0:T(4,128)}, u32[]{:S(2)}) copy-start(f32[2,4,512]{2,1,0:T(4,128)} %param.23) | copy-start | bytes 49156
  36.4 2.5 %copy-start.13 = (f32[2,512]{1,0:T(2,128)S(1)}, f32[2,512]{1,0:T(2,128)}, u32[]{:S(2)}) copy-start(f32[2,512]{1,0:T(2,128)} %param.24) | copy-start | bytes 12292
  36.5 2.5 %copy-start.3 = (bf16[2,512,544]{1,2,0:T(8,128)(2,1)S(1)}, bf16[2,512,544]{1,2,0:T(8,128)(2,1)}, u32[]{:S(2)}) copy-start(bf16[2,512,544]{1,2,0:T(8,128)(2,1)} %param.26) | copy-start | bytes 3342340
  36.5 15.0 %copy-start.14 = (f32[2,512]{1,0:T(2,128)S(1)}, f32[2,512]{1,0:T(2,128)}, u32[]{:S(2)}) copy-start(f32[2,512]{1,0:T(2,128)} %param.28) | copy-start | bytes 12292
  36.5 15.0 %copy-start.5 = (bf16[2,512,512]{2,1,0:T(8,128)(2,1)S(1)}, bf16[2,512,512]{2,1,0:T(8,128)(2,1)}, u32[]{:S(2)}) copy-start(bf16[2,512,512]{2,1,0:T(8,128)(2,1)} %param.27) | copy-start | bytes 3145732
  36.5 15.2 %copy-start.10 = (f32[2,16,512]{2,1,0:T(8,128)S(1)}, f32[2,16,512]{2,1,0:T(8,128)}, u32[]{:S(2)}) copy-start(f32[2,16,512]{2,1,0:T(8,128)} %param.29) | copy-start | bytes 196612
  36.5 15.2 %copy-start.2 = (f32[2,8,16,512]{3,2,1,0:T(8,128)S(1)}, f32[2,8,16,512]{3,2,1,0:T(8,128)}, u32[]{:S(2)}) copy-start(f32[2,8,16,512]{3,2,1,0:T(8,128)} %param.31) | copy-start | bytes 1572868
  36.5 15.4 %copy-start.15 = (f32[2,512]{1,0:T(2,128)S(1)}, f32[2,512]{1,0:T(2,128)}, u32[]{:S(2)}) copy-start(f32[2,512]{1,0:T(2,128)} %param.30) | copy-start | bytes 12292
  105.6 28.3 %copy-start.9 = (bf16[8,2,2,128]{3,2,1,0:T(2,128)(2,1)}, bf16[8,2,2,128]{3,2,1,0:T(2,128)(2,1)S(1)}, u32[]{:S(2)}) copy-start(bf16[8,2,2,128]{3,2,1,0:T(2,128)(2,1)S(1)} %reshape.210) | copy-start | bytes 24580
  133.9 2.4 %copy-start.4 = (bf16[2,512,544]{1,2,0:T(8,128)(2,1)S(1)}, bf16[2,512,544]{1,2,0:T(8,128)(2,1)}, u32[]{:S(2)}) copy-start(bf16[2,512,544]{1,2,0:T(8,128)(2,1)} %param.26) | copy-start | bytes 3342340
  133.9 12.5 %copy-start.6 = (bf16[2,512,512]{2,1,0:T(8,128)(2,1)S(1)}, bf16[2,512,512]{2,1,0:T(8,128)(2,1)}, u32[]{:S(2)}) copy-start(bf16[2,512,512]{2,1,0:T(8,128)(2,1)} %param.27) | copy-start | bytes 3145732
  133.9 29.7 %copy-start.1 = (s32[8]{0:T(128)S(1)}, s32[8]{0:T(128)}, u32[]{:S(2)}) copy-start(s32[8]{0:T(128)} %param.36) | copy-start | bytes 100
